TPU v7x, 32 devices: a whole 2x2x4 slice. The times are simulated.
32 devices in a mesh: gx: 8 (over z, y), gy: 4 (over x, core).
Axes of the slice: x: 2, y: 2, z: 4, core: 2. Of those that a mesh axis runs over, the one named last changes fastest.
Arguments:
- block_input: bfloat16 [960, 8192], P('gx', 'gy'), may hold values from -6 to 6
- attn_gain: float32 [960], P('gx'), may hold values from 0.5 to 1.5
- query_weight: bfloat16 [960, 960], P('gx', 'gy'), may hold values from -2 to 2
- key_weight: bfloat16 [960, 320], P('gx', 'gy'), may hold values from -2 to 2
- value_weight: bfloat16 [960, 320], P('gx', 'gy'), may hold values from -0.1875 to 0.1875
- output_weight: bfloat16 [960, 960], P('gy', 'gx'), may hold values from -0.5 to 0.5
- ffn_gain: float32 [960], P('gx'), may hold values from 0.5 to 1.5
- gate_weight: bfloat16 [960, 2560], P('gx', 'gy'), may hold values from -0.1875 to 0.1875
- up_weight: bfloat16 [960, 2560], P('gx', 'gy'), may hold values from -0.1875 to 0.1875
- down_weight: bfloat16 [2560, 960], P('gy', 'gx'), may hold values from -0.125 to 0.125
- segment_ids: int32 [8, 1024], P('gx'), may hold values from 0 to 7, never falling along the last dimension, each value on 1 to 512 neighbouring positions
- out_cotangent: bfloat16 [960, 8192], P('gx', 'gy'), may hold values from -6 to 6
Outputs:
- block_output: bfloat16 [960, 8192], P('gx', 'gy')
- input_grad: float32 [960, 8192], P('gx', 'gy')
- grad_attngain: float32 [960], P('gx')
- grad_query: float32 [960, 960], P('gx', 'gy')
- grad_key: float32 [960, 320], P('gx', 'gy')
- grad_value: float32 [960, 320], P('gx', 'gy')
- grad_outproj: float32 [960, 960], P('gy', 'gx')
- grad_ffngain: float32 [960], P('gx')
- grad_gate: float32 [960, 2560], P('gx', 'gy')
- grad_up: float32 [960, 2560], P('gx', 'gy')
- grad_down: float32 [2560, 960], P('gy', 'gx')
Inputs may be any that keep to these rules, and one draw needn't show every extreme that they name: `segment_ids`: along each packed sequence the numbers never fall.
All inputs are finite; a program needn't handle non-finite values.
Results may differ from a plain program's by a relative error of at most 0.023.
The roundings to bfloat16 on the way count: a program that leaves them out, or rounds other values in their place, can miss the bound.
Values may be sent and summed in bfloat16 or wider, within the bound.
A program may use at most 256 MiB of HBM per device.

v0:
```python
import math
import jax
import jax.numpy as jnp
from jax import lax
from jax.sharding import PartitionSpec as P

D = 960
QUERY_HEADS = 15
KEY_VALUE_HEADS = 5
HEAD_SIZE = 64
PACKED_LENGTH = 1024
EPS = 1e-05
THETA = 10000.0


def product(left, right):
    return jnp.dot(
        left.astype(jnp.float32),
        right.astype(jnp.float32),
        preferred_element_type=jnp.float32,
        precision=lax.Precision.HIGHEST,
    )


def einsum_full(form, left, right):
    return jnp.einsum(
        form, left.astype(jnp.float32), right.astype(jnp.float32), precision=lax.Precision.HIGHEST
    )


def segment_positions(segments):
    row_index = jnp.arange(segments.shape[1], dtype=jnp.int32)[None, :]
    starts = jnp.concatenate(
        [jnp.ones((segments.shape[0], 1), dtype=jnp.bool_), segments[:, 1:] != segments[:, :-1]],
        axis=1,
    )
    seg_first = lax.cummax(jnp.where(starts, row_index, jnp.zeros_like(row_index)), axis=1)
    return row_index - seg_first


def rope_tables(positions, half_dim):
    frequency = jnp.exp(-math.log(THETA) * jnp.arange(half_dim, dtype=jnp.float32) / half_dim)
    angles = positions.astype(jnp.float32)[:, None] * frequency[None, :]
    return (jnp.cos(angles)[:, None, :], jnp.sin(angles)[:, None, :])


def rotate(values, cos_table, sine_table, rotate_direction):
    n_rows = values.shape[0]
    half_dim = cos_table.shape[-1]
    split_heads = values.reshape(n_rows, -1, 2 * half_dim)
    lower_half = split_heads[..., :half_dim]
    upper_half = split_heads[..., half_dim:]
    new_lower = lower_half * cos_table - rotate_direction * upper_half * sine_table
    new_upper = upper_half * cos_table + rotate_direction * lower_half * sine_table
    return jnp.concatenate([new_lower, new_upper], axis=-1).reshape(n_rows, -1)


def contract_rows(left_rows, right_rows):
    return product(left_rows.T, right_rows)


def width_sum(values):
    return lax.psum(values, "gx")


def norm_forward(values, gain):
    scale = lax.rsqrt(width_sum(jnp.sum(values * values, axis=1)) / D + EPS)
    return (scale, (values * scale[:, None] * gain[None, :]).astype(jnp.bfloat16))


def norm_backward(values, scale, gain, grad_normed):
    weighted = grad_normed * gain[None, :]
    inner = width_sum(jnp.sum(weighted * values, axis=1)) / D
    grad_values = scale[:, None] * weighted - values * (scale * scale * scale * inner)[:, None]
    gain_part = jnp.sum(grad_normed * values * scale[:, None], axis=0)
    return (grad_values, gain_part)


def project_in(local_rows, weight):
    gathered = lax.all_gather(local_rows, "gy", axis=0, tiled=True)
    full_width = lax.all_to_all(gathered, "gx", split_axis=0, concat_axis=1, tiled=True)
    full_weight = lax.all_gather(weight, "gx", axis=0, tiled=True)
    return (gathered, product(full_width, full_weight))


def project_out(local_rows, weight):
    gathered = lax.all_gather(local_rows, "gx", axis=0, tiled=True)
    return (
        gathered,
        lax.psum_scatter(
            product(gathered, weight).astype(jnp.bfloat16), "gy", scatter_dimension=0, tiled=True
        ).astype(jnp.float32),
    )


def to_heads(columns):
    return lax.all_to_all(columns, "gy", split_axis=0, concat_axis=1, tiled=True)


def from_heads(block):
    return lax.all_to_all(block, "gy", split_axis=1, concat_axis=0, tiled=True)


def head_scores(query_per_head, key_per_head, allowed):
    scores = einsum_full("qkgd,ckd->kgqc", query_per_head, key_per_head) * HEAD_SIZE ** (-0.5)
    return jnp.where(allowed[None, None], scores, -jnp.inf)


def shards(
    block_input,
    attn_gain,
    query_weight,
    key_weight,
    value_weight,
    output_weight,
    ffn_gain,
    gate_weight,
    up_weight,
    down_weight,
    segment_ids,
    out_cotangent,
):
    resid_in = block_input.T.astype(jnp.float32)
    cot_local = out_cotangent.T
    scale_one, normed_one = norm_forward(resid_in, attn_gain)
    width_query = query_weight.shape[1]
    width_key = key_weight.shape[1]
    qkv_weight = jnp.concatenate([query_weight, key_weight, value_weight], axis=1)
    normed_one_rows, qkv_sums = project_in(normed_one, qkv_weight)
    qkv_raw = qkv_sums.astype(jnp.bfloat16)
    query_raw = qkv_raw[:, :width_query]
    key_raw = qkv_raw[:, width_query : width_query + width_key]
    value_raw = qkv_raw[:, width_query + width_key :]
    query_block = to_heads(query_raw)
    key_full, value_expanded = (
        lax.all_gather(key_raw, "gy", axis=1, tiled=True),
        lax.all_gather(value_raw, "gy", axis=1, tiled=True),
    )
    block_row_slab = query_block.shape[0]
    query_groups = QUERY_HEADS // KEY_VALUE_HEADS
    query_start = lax.axis_index("gy") * block_row_slab
    seq_start = query_start // PACKED_LENGTH * PACKED_LENGTH
    positions = segment_positions(segment_ids).reshape(-1)
    seg_flat = segment_ids.reshape(-1)
    cos_all, sine_all = rope_tables(positions, HEAD_SIZE // 2)
    cos_query = lax.dynamic_slice_in_dim(cos_all, query_start, block_row_slab, 0)
    sine_query = lax.dynamic_slice_in_dim(sine_all, query_start, block_row_slab, 0)
    key_rotated = rotate(key_full.astype(jnp.float32), cos_all, sine_all, 1.0).astype(jnp.bfloat16)
    query_rotated = rotate(query_block.astype(jnp.float32), cos_query, sine_query, 1.0).astype(
        jnp.bfloat16
    )
    seg_query = lax.dynamic_slice_in_dim(seg_flat, query_start, block_row_slab, 0)
    query_index = query_start - seq_start + jnp.arange(block_row_slab, dtype=jnp.int32)
    key_index = jnp.arange(PACKED_LENGTH, dtype=jnp.int32)
    allowed = (seg_query[:, None] == seg_flat[None, :]) & (
        key_index[None, :] <= query_index[:, None]
    )
    query_per_head = query_rotated.reshape(block_row_slab, KEY_VALUE_HEADS, query_groups, HEAD_SIZE)
    key_per_head = key_rotated.reshape(PACKED_LENGTH, KEY_VALUE_HEADS, HEAD_SIZE)
    value_per_head = value_expanded.reshape(PACKED_LENGTH, KEY_VALUE_HEADS, HEAD_SIZE)
    scores = head_scores(query_per_head, key_per_head, allowed)
    row_top = jnp.max(scores, axis=-1, keepdims=True)
    log_total = row_top + jnp.log(jnp.sum(jnp.exp(scores - row_top), axis=-1, keepdims=True))
    prob_half = jnp.exp(scores - log_total).astype(jnp.bfloat16)
    mixed = einsum_full("kgqc,ckd->qkgd", prob_half, value_per_head)
    attn_block = mixed.reshape(block_row_slab, -1).astype(jnp.bfloat16)
    attn_rows = from_heads(attn_block)
    attn_gathered, attn_sum = project_out(attn_rows, output_weight)
    hidden_in = resid_in + attn_sum
    scale_two, normed_two = norm_forward(hidden_in, ffn_gain)
    width_ff = gate_weight.shape[1]
    gate_up = jnp.concatenate([gate_weight, up_weight], axis=1)
    normed_two_rows, gate_sums = project_in(normed_two, gate_up)
    gate_pre = gate_sums[:, :width_ff]
    up_pre = gate_sums[:, width_ff:]
    hidden = (jax.nn.silu(gate_pre) * up_pre).astype(jnp.bfloat16)
    hidden_gathered, ffn_sum = project_out(hidden, down_weight)
    block_output = (hidden_in + ffn_sum).astype(jnp.bfloat16)
    cot_rows, hidden_grad = project_in(cot_local, down_weight.T)
    grad_down = contract_rows(lax.all_gather(hidden, "gx", axis=0, tiled=True), cot_rows)
    gate_sigmoid = jax.nn.sigmoid(gate_pre)
    gate_back = (
        hidden_grad * up_pre * gate_sigmoid * (1.0 + gate_pre * (1.0 - gate_sigmoid))
    ).astype(jnp.bfloat16)
    up_back = (hidden_grad * gate_pre * gate_sigmoid).astype(jnp.bfloat16)
    gate_up_rows, normed_two_grad = project_out(
        jnp.concatenate([gate_back, up_back], axis=1), gate_up.T
    )
    grad_gate_up = contract_rows(normed_two_rows, gate_up_rows)
    hidden_in_grad, gain_two_part = norm_backward(hidden_in, scale_two, ffn_gain, normed_two_grad)
    hidden_in_grad = hidden_in_grad + cot_local.astype(jnp.float32)
    hidden_in_half = hidden_in_grad.astype(jnp.bfloat16)
    grad_rows, attn_grad = project_in(hidden_in_half, output_weight.T)
    grad_outproj = contract_rows(attn_gathered, grad_rows)
    block_gradient = to_heads(attn_grad.astype(jnp.bfloat16))
    head_gradient = block_gradient.reshape(block_row_slab, KEY_VALUE_HEADS, query_groups, HEAD_SIZE)
    scores = head_scores(query_per_head, key_per_head, allowed)
    prob_full = jnp.exp(scores - log_total)
    prob_half = prob_full.astype(jnp.bfloat16)
    prob_grad = einsum_full("qkgd,ckd->kgqc", head_gradient, value_per_head)
    row_dot = jnp.sum(prob_full * prob_grad, axis=-1, keepdims=True)
    score_grad = (prob_full * (prob_grad - row_dot) * HEAD_SIZE ** (-0.5)).astype(jnp.bfloat16)
    query_grad = einsum_full("kgqc,ckd->qkgd", score_grad, key_per_head).reshape(block_row_slab, -1)
    key_grad = einsum_full("kgqc,qkgd->ckd", score_grad, query_per_head).reshape(PACKED_LENGTH, -1)
    value_grad = einsum_full("kgqc,qkgd->ckd", prob_half, head_gradient).reshape(PACKED_LENGTH, -1)
    query_back = rotate(query_grad, cos_query, sine_query, -1.0).astype(jnp.bfloat16)
    key_grad_all = rotate(key_grad, cos_all, sine_all, -1.0)
    key_back, value_back = (
        lax.psum_scatter(
            key_grad_all.astype(jnp.bfloat16), "gy", scatter_dimension=1, tiled=True
        ).astype(jnp.float32),
        lax.psum_scatter(
            value_grad.astype(jnp.bfloat16), "gy", scatter_dimension=1, tiled=True
        ).astype(jnp.float32),
    )
    query_cols = from_heads(query_back)
    qkv_grad = jnp.concatenate(
        [query_cols, key_back.astype(jnp.bfloat16), value_back.astype(jnp.bfloat16)], axis=1
    )
    qkv_grad_rows, normed_one_grad = project_out(qkv_grad, qkv_weight.T)
    grad_qkv = contract_rows(normed_one_rows, qkv_grad_rows)
    input_grad, gain_one_part = norm_backward(resid_in, scale_one, attn_gain, normed_one_grad)
    input_grad = input_grad + hidden_in_grad
    grad_attngain, grad_ffngain = lax.psum((gain_one_part, gain_two_part), "gy")
    grad_query = grad_qkv[:, :width_query]
    grad_key = grad_qkv[:, width_query : width_query + width_key]
    grad_value = grad_qkv[:, width_query + width_key :]
    grad_gate = grad_gate_up[:, :width_ff]
    grad_up = grad_gate_up[:, width_ff:]
    return (
        block_output.T,
        input_grad.T,
        grad_attngain,
        grad_query,
        grad_key,
        grad_value,
        grad_outproj,
        grad_ffngain,
        grad_gate,
        grad_up,
        grad_down,
    )


def solution(mesh):
    return jax.shard_map(
        shards,
        mesh=mesh,
        in_specs=(
            P("gx", "gy"),
            P("gx"),
            P("gx", "gy"),
            P("gx", "gy"),
            P("gx", "gy"),
            P("gy", "gx"),
            P("gx"),
            P("gx", "gy"),
            P("gx", "gy"),
            P("gy", "gx"),
            P("gx", None),
            P("gx", "gy"),
        ),
        out_specs=(
            P("gx", "gy"),
            P("gx", "gy"),
            P("gx"),
            P("gx", "gy"),
            P("gx", "gy"),
            P("gx", "gy"),
            P("gy", "gx"),
            P("gx"),
            P("gx", "gy"),
            P("gx", "gy"),
            P("gy", "gx"),
        ),
        check_vma=False,
    )
```

profile of v0, /device:TPU:0, one launch (start us, length us, event | category | flops | bytes accessed | tf_op | source)
XLA Modules:
  0.0 1488.6 jit_solution(9215844757252421216)
XLA Ops:
  8.4 23.4 %psum.42 = f32[2048]{0:T(1024)S(1)} all-reduce(f32[2048]{0:T(1024)S(1)} %fusion.35), channel_id=1, replica_groups=mesh['gx'=8,'gy'=4] {'gx'}, use_global_device_ids=true, to_apply=%region_1.0 | all-reduce | flops 2048 | bytes 16384 | tf_op jit(solution)/shard_map/psum | solution.py:63
  33.8 19.2 %all-gather.12.cloned.1.call-done = bf16[8192,120]{0,1:T(8,128)(2,1)} async-done(((bf16[2048,120]{0,1:T(8,128)(2,1)}), bf16[8192,120]{0,1:T(8,128)(2,1)}) %all-gather.12.cloned.1.call-update) | async-done | bytes 1966096 | tf_op jit(solution)/shard_map/all_gather | solution.py:80
  56.0 5.7 all-to-all-start
  62.7 67.0 %all-gather = bf16[8,120,400]{1,2,0:T(8,128)(2,1)S(1)} all-gather(bf16[1,120,400]{1,2,0:T(8,128)(2,1)S(1)} %fusion.41), channel_id=1, replica_groups=mesh['gx'=8,'gy'=4] {'gx'}, dimensions={0}, use_global_device_ids=true | all-gather | bytes 864000 | tf_op jit(solution)/shard_map/all_gather | solution.py:82
  136.2 3.5 all-to-all-start.1
  139.8 12.8 all_gather.46
  152.5 8.0 all_gather.45
  161.1 6.8 fusion.52
  168.0 7.5 exponential_reduce_fusion
  175.5 8.0 fusion.16
  183.5 10.9 all_to_all.137
  195.3 68.4 %all-gather.14.cloned.1.call-done = bf16[8192,240]{0,1:T(8,128)(2,1)} async-done(((bf16[1024,240]{0,1:T(8,128)(2,1)}), bf16[8192,240]{0,1:T(8,128)(2,1)}) %all-gather.14.cloned.1.call-update) | async-done | bytes 3932176 | tf_op jit(solution)/shard_map/all_gather | solution.py:87
  263.7 4.1 convolution_convert_fusion
  268.4 28.6 %reduce-scatter.7.cloned.1.call-done = bf16[2048,120]{0,1:T(8,128)(2,1)} async-done(((bf16[8192,120]{0,1:T(8,128)(2,1)}), bf16[2048,120]{0,1:T(8,128)(2,1)}) %reduce-scatter.7.cloned.1.call-update) | async-done | bytes 491536 | tf_op jit(solution)/shard_map/reduce_scatter | solution.py:90
  298.3 21.7 %psum.43 = f32[2048]{0:T(1024)S(1)} all-reduce(f32[2048]{0:T(1024)S(1)} %multiply_reduce_fusion), channel_id=1, replica_groups=mesh['gx'=8,'gy'=4] {'gx'}, use_global_device_ids=true, to_apply=%region_8.9 | all-reduce | flops 2048 | bytes 16384 | tf_op jit(solution)/shard_map/psum | solution.py:63
  322.6 17.7 %all-gather.16.cloned.1.call-done = bf16[8192,120]{0,1:T(8,128)(2,1)} async-done(((bf16[2048,120]{0,1:T(8,128)(2,1)}), bf16[8192,120]{0,1:T(8,128)(2,1)}) %all-gather.16.cloned.1.call-update) | async-done | bytes 1966096 | tf_op jit(solution)/shard_map/all_gather | solution.py:80
  343.3 5.6 all-to-all-start.3
  349.8 13.8 all-gather.22.cloned.1.call-done
  366.6 38.2 %all-to-all-done.3 = bf16[8,1024,120]{1,2,0:T(8,128)(2,1)} async-done(((bf16[8,1024,120]{1,2,0:T(8,128)(2,1)}), bf16[8,1024,120]{1,2,0:T(8,128)(2,1)}, u32[]{:S(2)}, u32[]{:S(2)}) %all-to-all-start.3) | async-done | bytes 1966112 | tf_op jit(solution)/shard_map/all_to_all | solution.py:81
  404.8 4.3 all-to-all-start.4
  409.9 36.0 %all-gather.18.cloned.1.call-done = bf16[960,1280]{1,0:T(8,128)(2,1)} async-done(((bf16[120,1280]{1,0:T(8,128)(2,1)}), bf16[960,1280]{1,0:T(8,128)(2,1)}) %all-gather.18.cloned.1.call-update) | async-done | bytes 2457616 | tf_op jit(solution)/shard_map/all_gather | solution.py:82
  445.9 7.5 fusion.53
  453.4 45.1 %all-gather.24.cloned.1.call-done = bf16[960,640]{1,0:T(8,128)(2,1)} async-done(((bf16[120,640]{1,0:T(8,128)(2,1)}), bf16[960,640]{1,0:T(8,128)(2,1)}) %all-gather.24.cloned.1.call-update) | async-done | bytes 1228816 | tf_op jit(solution)/shard_map/all_gather | solution.py:82
  498.5 7.3 multiply_convert_fusion.1
  507.6 400.4 %all-gather.26.cloned.1.call-done = bf16[8192,1280]{1,0:T(8,128)(2,1)} async-done(((bf16[1024,1280]{1,0:T(8,128)(2,1)}), bf16[8192,1280]{1,0:T(8,128)(2,1)}) %all-gather.26.cloned.1.call-update) | async-done | bytes 20971536 | tf_op jit(solution)/shard_map/all_gather | solution.py:87
  908.0 14.8 convolution_convert_fusion.3
  922.9 30.5 %reduce-scatter.11.cloned.1.call-done = bf16[2048,120]{0,1:T(8,128)(2,1)} async-done(((bf16[8192,120]{0,1:T(8,128)(2,1)}), bf16[2048,120]{0,1:T(8,128)(2,1)}) %reduce-scatter.11.cloned.1.call-update) | async-done | bytes 491536 | tf_op jit(solution)/shard_map/reduce_scatter | solution.py:90
  955.4 22.4 %psum.44 = f32[2048]{0:T(1024)} all-reduce(f32[2048]{0:T(1024)S(1)} %get-tuple-element.56), channel_id=1, replica_groups=mesh['gx'=8,'gy'=4] {'gx'}, use_global_device_ids=true, to_apply=%region_12.13 | all-reduce | flops 2048 | bytes 16384 | tf_op jit(solution)/shard_map/psum | solution.py:63
  980.8 18.3 %all-gather.28.cloned.1.call-done = bf16[8192,120]{0,1:T(8,128)(2,1)} async-done(((bf16[2048,120]{0,1:T(8,128)(2,1)}), bf16[8192,120]{0,1:T(8,128)(2,1)}) %all-gather.28.cloned.1.call-update) | async-done | bytes 1966096 | tf_op jit(solution)/shard_map/all_gather | solution.py:80
  1002.1 5.5 all-to-all-start.5
  1009.2 67.3 %all_gather.55 = bf16[960,240]{1,0:T(8,128)(2,1)} all-gather(bf16[120,240]{1,0:T(8,128)(2,1)} %bitcast.221), channel_id=1, replica_groups=mesh['gx'=8,'gy'=4] {'gx'}, dimensions={0}, use_global_device_ids=true | all-gather | bytes 518400 | tf_op jit(solution)/shard_map/all_gather | solution.py:82
  1078.8 10.9 all_to_all.138
  1089.7 8.9 fusion.13
  1098.6 7.8 fusion.54
  1106.4 25.3 %fusion.3 = bf16[5,3,256,1024]{2,3,1,0:T(8,128)(2,1)} fusion(f32[5,1024,256,3]{2,1,3,0:T(8,128)} %fusion.54, f32[5,3,256,1024]{2,3,1,0:T(8,128)} %get-tuple-element.86, f32[5,3,256]{2,1,0:T(4,128)S(1)} %log_add_fusion), kind=kOutput, calls=%fused_computation.5 | output fusion | flops 27529984 | bytes 39336960 | tf_op jit(solution)/shard_map/sub | solution.py:202
  1131.7 5.7 convolution_bitcast_fusion
  1138.6 4.7 fusion.39
  1143.5 10.9 all_to_all.139
  1154.4 5.2 reduce-scatter.13.cloned.1.call-done
  1162.4 101.9 %all-gather.30.cloned.1.call-done = bf16[8192,400]{0,1:T(8,128)(2,1)} async-done(((bf16[1024,400]{0,1:T(8,128)(2,1)}), bf16[8192,400]{0,1:T(8,128)(2,1)}) %all-gather.30.cloned.1.call-update) | async-done | bytes 6553616 | tf_op jit(solution)/shard_map/all_gather | solution.py:87
  1264.3 5.4 convolution_convert_fusion.1
  1269.8 145.3 %all-gather.20.cloned.1.call-done = bf16[8192,640]{1,0:T(8,128)(2,1)} async-done(((bf16[1024,640]{1,0:T(8,128)(2,1)}), bf16[8192,640]{1,0:T(8,128)(2,1)}) %all-gather.20.cloned.1.call-update) | async-done | bytes 10485776 | tf_op jit(solution)/shard_map/all_gather | solution.py:87
  1415.0 9.3 convolution_convert_fusion.2
  1424.4 7.2 fusion.58
  1431.6 8.9 fusion.57
  1448.1 6.8 all-reduce
  1454.8 20.8 %psum.45 = f32[2048]{0:T(1024)S(1)} all-reduce(f32[2048]{0:T(1024)S(1)} %get-tuple-element.58), channel_id=1, replica_groups=mesh['gx'=8,'gy'=4] {'gx'}, use_global_device_ids=true, to_apply=%region_18.19 | all-reduce | flops 2048 | bytes 16384 | tf_op jit(solution)/shard_map/psum | solution.py:63
  1475.6 3.3 reduce-scatter.9.cloned.1.call-done
  (161 shorter events, 55.7 us)
Async XLA Ops:
  7.2 45.8 %all-gather.12.cloned.1.call-start = ((), (), s32[]{:S(2)}) async-start(), calls=%async_computation.14 | async-start | bytes 2457600 | tf_op jit(solution)/shard_map/all_gather | solution.py:80
  56.0 5.7 copy-start.22
  56.0 6.5 copy-start.21
  56.0 6.6 copy-start.16
  56.0 6.6 copy-start.18
  56.0 76.8 %all-to-all-start = ((bf16[8,1024,120]{1,2,0:T(8,128)(2,1)}), bf16[8,1024,120]{1,2,0:T(8,128)(2,1)}, u32[]{:S(2)}, u32[]{:S(2)}) async-start(bf16[8,1024,120]{1,2,0:T(8,128)(2,1)} %bitcast.187), calls=%async_computation | async-start | bytes 3932160 | tf_op jit(solution)/shard_map/all_to_all | solution.py:81
  136.2 24.6 %all-to-all-start.1 = ((bf16[4,256,240]{1,2,0:T(8,128)(2,1)}), bf16[4,256,240]{1,2,0:T(8,128)(2,1)S(1)}, u32[]{:S(2)}, u32[]{:S(2)}) async-start(bf16[4,256,240]{1,2,0:T(8,128)(2,1)} %bitcast.189), calls=%async_computation.1 | async-start | bytes 983040 | tf_op jit(solution)/shard_map/all_to_all | solution.py:97
  139.7 124.0 %all-gather.14.cloned.1.call-start = ((), (), s32[]{:S(2)}) async-start(), calls=%async_computation.15 | async-start | bytes 4423680 | tf_op jit(solution)/shard_map/all_gather | solution.py:87
  175.5 88.2 %copy-start.12 = (bf16[240,120]{1,0:T(8,128)(2,1)S(1)}, bf16[240,120]{1,0:T(8,128)(2,1)}, u32[]{:S(2)}) copy-start(bf16[240,120]{1,0:T(8,128)(2,1)} %param.17) | copy-start | bytes 172804
  195.3 101.8 %copy-start = (bf16[120,2048]{1,0:T(8,128)(2,1)S(1)}, bf16[120,2048]{1,0:T(8,128)(2,1)}, u32[]{:S(2)}) copy-start(bf16[120,2048]{1,0:T(8,128)(2,1)} %param.12) | copy-start | bytes 1474564
  195.3 101.8 %reduce-scatter.7.cloned.1.call-start = ((), (), s32[]{:S(2)}) async-start(), calls=%async_computation.16 | async-start | bytes 2457600 | tf_op jit(solution)/shard_map/reduce_scatter | solution.py:90
  267.9 52.1 %copy-start.23 = (f32[120]{0:T(128)S(1)}, f32[120]{0:T(128)}, u32[]{:S(2)}) copy-start(f32[120]{0:T(128)} %param.18) | copy-start | bytes 1444
  267.9 72.4 %all-gather.16.cloned.1.call-start = ((), (), s32[]{:S(2)}) async-start(), calls=%async_computation.17 | async-start | bytes 2457600 | tf_op jit(solution)/shard_map/all_gather | solution.py:80
  320.0 23.3 %copy-start.20 = (f32[2048]{0:T(1024)}, f32[2048]{0:T(1024)S(1)}, u32[]{:S(2)}) copy-start(f32[2048]{0:T(1024)S(1)} %psum.43) | copy-start | bytes 24580
  322.0 41.5 %all-gather.22.cloned.1.call-start = ((), (), s32[]{:S(2)}) async-start(), calls=%async_computation.21 | async-start | bytes 2457600 | tf_op jit(solution)/shard_map/all_gather | solution.py:80
  343.3 5.7 copy-start.13
  343.3 5.7 copy-start.14
  343.3 61.5 %all-to-all-start.3 = ((bf16[8,1024,120]{1,2,0:T(8,128)(2,1)}), bf16[8,1024,120]{1,2,0:T(8,128)(2,1)}, u32[]{:S(2)}, u32[]{:S(2)}) async-start(bf16[8,1024,120]{1,2,0:T(8,128)(2,1)} %bitcast.198), calls=%async_computation.4 | async-start | bytes 3932160 | tf_op jit(solution)/shard_map/all_to_all | solution.py:81
  348.9 97.0 %all-gather.18.cloned.1.call-start = ((), (), s32[]{:S(2)}) async-start(), calls=%async_computation.18 | async-start | bytes 2764800 | tf_op jit(solution)/shard_map/all_gather | solution.py:82
  404.8 93.8 %all-to-all-start.4 = ((bf16[8,1024,120]{1,2,0:T(8,128)(2,1)}), bf16[8,1024,120]{1,2,0:T(8,128)(2,1)}, u32[]{:S(2)}, u32[]{:S(2)}) async-start(bf16[8,1024,120]{1,2,0:T(8,128)(2,1)} %bitcast.197), calls=%async_computation.6 | async-start | bytes 3932160 | tf_op jit(solution)/shard_map/all_to_all | solution.py:81
  409.1 89.4 %all-gather.24.cloned.1.call-start = ((), (), s32[]{:S(2)}) async-start(), calls=%async_computation.22 | async-start | bytes 1382400 | tf_op jit(solution)/shard_map/all_gather | solution.py:82
  409.9 498.1 %all-gather.26.cloned.1.call-start = ((), (), s32[]{:S(2)}) async-start(), calls=%async_computation.23 | async-start | bytes 23592960 | tf_op jit(solution)/shard_map/all_gather | solution.py:87
  507.5 400.5 %copy-start.9 = (bf16[120,1280]{1,0:T(8,128)(2,1)S(1)}, bf16[120,1280]{1,0:T(8,128)(2,1)}, u32[]{:S(2)}) copy-start(bf16[120,1280]{1,0:T(8,128)(2,1)} %copy-done.8) | copy-start | bytes 921604
  507.5 445.9 %copy-start.3 = (bf16[2048,120]{0,1:T(8,128)(2,1)S(1)}, bf16[2048,120]{0,1:T(8,128)(2,1)}, u32[]{:S(2)}) copy-start(bf16[2048,120]{0,1:T(8,128)(2,1)} %reduce-scatter.7.cloned.1.call-done) | copy-start | bytes 1474564
  507.5 445.8 %reduce-scatter.11.cloned.1.call-start = ((), (), s32[]{:S(2)}) async-start(), calls=%async_computation.24 | async-start | bytes 2457600 | tf_op jit(solution)/shard_map/reduce_scatter | solution.py:90
  922.8 55.8 %copy-start.6 = (bf16[120,2048]{1,0:T(8,128)(2,1)S(1)}, bf16[120,2048]{1,0:T(8,128)(2,1)}, u32[]{:S(2)}) copy-start(bf16[120,2048]{1,0:T(8,128)(2,1)} %param.23) | copy-start | bytes 1474564
  922.8 76.2 %all-gather.28.cloned.1.call-start = ((), (), s32[]{:S(2)}) async-start(), calls=%async_computation.25 | async-start | bytes 2457600 | tf_op jit(solution)/shard_map/all_gather | solution.py:80
  1002.1 74.4 %all-to-all-start.5 = ((bf16[8,1024,120]{1,2,0:T(8,128)(2,1)}), bf16[8,1024,120]{1,2,0:T(8,128)(2,1)}, u32[]{:S(2)}, u32[]{:S(2)}) async-start(bf16[8,1024,120]{1,2,0:T(8,128)(2,1)} %bitcast.199), calls=%async_computation.8 | async-start | bytes 3932160 | tf_op jit(solution)/shard_map/all_to_all | solution.py:81
  1007.6 146.8 %reduce-scatter.15.cloned.1.call-start = ((), (), s32[]{:S(2)}) async-start(), calls=%async_computation.27 | async-start | bytes 819200 | tf_op jit(solution)/shard_map/reduce_scatter | solution.py:212
  1106.3 53.2 %reduce-scatter.13.cloned.1.call-start = ((), (), s32[]{:S(2)}) async-start(), calls=%async_computation.26 | async-start | bytes 819200 | tf_op jit(solution)/shard_map/reduce_scatter | solution.py:209
  1131.7 5.7 copy-start.11
  1138.5 4.7 copy-start.15
  1138.5 125.7 %all-gather.30.cloned.1.call-start = ((), (), s32[]{:S(2)}) async-start(), calls=%async_computation.28 | async-start | bytes 7372800 | tf_op jit(solution)/shard_map/all_gather | solution.py:87
  1154.3 110.0 %copy-start.17 = (bf16[120,80]{0,1:T(8,128)(2,1)S(1)}, bf16[120,80]{0,1:T(8,128)(2,1)}, u32[]{:S(2)}) copy-start(bf16[120,80]{0,1:T(8,128)(2,1)} %param.16) | copy-start | bytes 57604
  1154.3 110.0 %copy-start.19 = (bf16[120,80]{0,1:T(8,128)(2,1)S(1)}, bf16[120,80]{0,1:T(8,128)(2,1)}, u32[]{:S(2)}) copy-start(bf16[120,80]{0,1:T(8,128)(2,1)} %param.15) | copy-start | bytes 57604
  1161.5 253.5 %all-gather.20.cloned.1.call-start = ((), (), s32[]{:S(2)}) async-start(), calls=%async_computation.19 | async-start | bytes 11796480 | tf_op jit(solution)/shard_map/all_gather | solution.py:87
  1162.1 252.9 %copy-start.10 = (bf16[640,120]{0,1:T(8,128)(2,1)S(1)}, bf16[640,120]{0,1:T(8,128)(2,1)}, u32[]{:S(2)}) copy-start(bf16[640,120]{0,1:T(8,128)(2,1)} %param.21) | copy-start | bytes 460804
  1162.1 284.4 %reduce-scatter.17.cloned.1.call-start = ((), (), s32[]{:S(2)}) async-start(), calls=%async_computation.29 | async-start | bytes 2457600 | tf_op jit(solution)/shard_map/reduce_scatter | solution.py:90
  1269.7 209.2 %reduce-scatter.9.cloned.1.call-start = ((), (), s32[]{:S(2)}) async-start(), calls=%async_computation.20 | async-start | bytes 2457600 | tf_op jit(solution)/shard_map/reduce_scatter | solution.py:90
  1424.4 7.2 copy-start.4
  1424.4 18.8 %slice-start = ((s8[6553600]{0:T(1024)(128)(4,1)}), s8[4194304]{0:T(1024)(128)(4,1)S(1)}, s32[]{:S(2)}) async-start(s8[6553600]{0:T(1024)(128)(4,1)} %bitcast.190), calls=%async_computation.30 | async-start | bytes 8388608
  1431.6 9.8 copy-start.1
  1431.6 9.8 copy-start.5
  1431.6 11.6 slice-start.1
  1443.2 3.4 copy-start.25
  1443.2 4.8 copy-start.26
  1443.2 35.7 %copy-start.7 = (bf16[2048,120]{0,1:T(8,128)(2,1)S(1)}, bf16[2048,120]{0,1:T(8,128)(2,1)}, u32[]{:S(2)}) copy-start(bf16[2048,120]{0,1:T(8,128)(2,1)} %reduce-scatter.11.cloned.1.call-done) | copy-start | bytes 1474564
  1443.2 35.7 %copy-start.24 = (f32[120]{0:T(128)S(1)}, f32[120]{0:T(128)}, u32[]{:S(2)}) copy-start(f32[120]{0:T(128)} %param.18) | copy-start | bytes 1444
  (2 other events, 2.6 us)
Sparse Core Ops, SparseCore 0:
  33.9 19.0 all-gather.11
  195.4 68.2 all-gather.13
  268.0 28.9 reduce-scatter.6
  322.1 18.0 all-gather.15
  341.7 21.8 all-gather.21
  366.1 79.7 all-gather.17
  448.1 50.4 all-gather.23
  507.7 400.3 all-gather.25
  923.0 30.3 reduce-scatter.10
  980.9 18.1 all-gather.27
  1106.5 20.9 reduce-scatter.14
  1138.6 20.8 reduce-scatter.12
  1162.3 101.8 all-gather.29
  1266.3 148.6 all-gather.19
  1417.5 28.5 reduce-scatter.16
  1448.5 30.3 reduce-scatter.8
where the time goes:
time: 1500 us; the launch traced here: 1490 us
  waiting for transfers between devices  974 us (65%)
  blocking collectives  283 us (19%)
  matrix products  115 us (8%)
  other arithmetic  56.8 us (4%)
  starting transfers between devices  26 us (2%)
  local copies, waits for them, and re-layouts  19.8 us (1%)
    all_gather x4, waiting for transfers between devices, project_out(): gathered = lax.all_gather(local_rows, 'gx', axis=0, tiled=True)  716 us
    all_gather x2, blocking collectives, project_in(): full_weight = lax.all_gather(weight, 'gx', axis=0, tiled=True)  134 us
    psum x4, blocking collectives, width_sum(): return lax.psum(values, 'gx')  88.3 us
    all_gather x2, waiting for transfers between devices, project_in(): full_weight = lax.all_gather(weight, 'gx', axis=0, tiled=True)  81.1 us
    dot_general x12, matrix products, product(): jnp.dot(left.astype(jnp.float32), right.astype(jnp.float32), preferred_el...  73.2 us
    all_gather x4, waiting for transfers between devices, project_in(): gathered = lax.all_gather(local_rows, 'gy', axis=0, tiled=True)  68.9 us
    reduce_scatter x4, waiting for transfers between devices, project_out(): lax.psum_scatter(product(gathered, weight).astype(jnp.bfloat16), 'gy', sc...  62.4 us
    dot_general x6, matrix products, einsum_full(): jnp.einsum(form, left.astype(jnp.float32), right.astype(jnp.float32), pre...  41.8 us
  transfers between devices with their start and end apart: 21, of which 15 were waited for; matrix products, arithmetic and copies ran while one was open for 6% of the time, Pallas kernels for 0%

commit v1 on v0

--- a/solution.py
+++ b/solution.py
@@ -1,3 +1,4 @@
+import functools
 import math
 import jax
 import jax.numpy as jnp
@@ -11,6 +12,14 @@
 PACKED_LENGTH = 1024
 EPS = 1e-05
 THETA = 10000.0
+
+
+def groups_update(local_x, comm_axis):
+    state_now = lax.all_gather(local_x, axis_name=comm_axis)
+    return jnp.sum(state_now, 0)
+
+
+post_steps_all = functools.partial(groups_update, comm_axis="gx")
 
 
 def product(left, right):
@@ -60,7 +69,7 @@
 
 
 def width_sum(values):
-    return lax.psum(values, "gx")
+    return post_steps_all(values)
 
 
 def norm_forward(values, gain):

time: 1500 us -> 1550 us (1.033)
  blocking collectives: 283 us -> 320 us
    all_gather x0 -> x4, blocking collectives: none -> 126 us  [groups_update(): state_now = lax.all_gather(local_x, axis_name=comm_axis)]
    psum x4 -> x0, blocking collectives: 88.3 us -> none  [width_sum(): return lax.psum(values, 'gx')]
  transfers between devices with their start and end apart: 21 -> 21, of which waited for: 15 -> 14; matrix products, arithmetic and copies ran while one was open for 6% -> 6% of each run, Pallas kernels for 0% -> 0%
where the time goes in v1:
time: 1550 us; the launch traced here: 1540 us
  waiting for transfers between devices  981 us (63%)
  blocking collectives  320 us (21%)
  matrix products  115 us (7%)
  other arithmetic  58.3 us (4%)
  starting transfers between devices  26.1 us (2%)
  local copies, waits for them, and re-layouts  21.3 us (1%)
    all_gather x4, waiting for transfers between devices, project_out(): gathered = lax.all_gather(local_rows, 'gx', axis=0, tiled=True)  716 us
    all_gather x2, blocking collectives, project_in(): full_weight = lax.all_gather(weight, 'gx', axis=0, tiled=True)  134 us
    all_gather x4, blocking collectives, groups_update(): state_now = lax.all_gather(local_x, axis_name=comm_axis)  126 us
    all_gather x2, waiting for transfers between devices, project_in(): full_weight = lax.all_gather(weight, 'gx', axis=0, tiled=True)  81.1 us
    all_gather x4, waiting for transfers between devices, project_in(): gathered = lax.all_gather(local_rows, 'gy', axis=0, tiled=True)  79.9 us
    dot_general x12, matrix products, product(): jnp.dot(left.astype(jnp.float32), right.astype(jnp.float32), preferred_el...  73.2 us
    reduce_scatter x4, waiting for transfers between devices, project_out(): lax.psum_scatter(product(gathered, weight).astype(jnp.bfloat16), 'gy', sc...  59.5 us
    dot_general x6, matrix products, einsum_full(): jnp.einsum(form, left.astype(jnp.float32), right.astype(jnp.float32), pre...  41.8 us
  transfers between devices with their start and end apart: 21, of which 14 were waited for; matrix products, arithmetic and copies ran while one was open for 6% of the time, Pallas kernels for 0%

profile of v1, /device:TPU:0, one launch (start us, length us, event | category | flops | bytes accessed | tf_op | source)
XLA Modules:
  0.0 1536.6 jit_solution(5018626054229320383)
XLA Ops:
  8.4 32.4 %all-gather = f32[16384]{0:T(1024)S(1)} all-gather(f32[2048]{0:T(1024)S(1)} %fusion.35), channel_id=2, replica_groups=mesh['gx'=8,'gy'=4] {'gx'}, dimensions={0}, use_global_device_ids=true | all-gather | bytes 73728 | tf_op jit(solution)/shard_map/all_gather | solution.py:18
  42.8 22.9 %all-gather.16.cloned.1.call-done = bf16[8192,120]{0,1:T(8,128)(2,1)} async-done(((bf16[2048,120]{0,1:T(8,128)(2,1)}), bf16[8192,120]{0,1:T(8,128)(2,1)}) %all-gather.16.cloned.1.call-update) | async-done | bytes 1966096 | tf_op jit(solution)/shard_map/all_gather | solution.py:89
  68.7 5.7 all-to-all-start
  75.3 67.0 %all-gather.4 = bf16[8,120,400]{1,2,0:T(8,128)(2,1)S(1)} all-gather(bf16[1,120,400]{1,2,0:T(8,128)(2,1)S(1)} %fusion.41), channel_id=1, replica_groups=mesh['gx'=8,'gy'=4] {'gx'}, dimensions={0}, use_global_device_ids=true | all-gather | bytes 864000 | tf_op jit(solution)/shard_map/all_gather | solution.py:91
  148.9 3.5 all-to-all-start.1
  152.4 12.8 all_gather.72
  165.2 8.0 all_gather.71
  173.8 6.8 fusion.52
  180.6 7.5 exponential_reduce_fusion
  188.2 8.0 fusion.16
  196.2 10.9 all_to_all.137
  208.4 67.9 %all-gather.18.cloned.1.call-done = bf16[8192,240]{0,1:T(8,128)(2,1)} async-done(((bf16[1024,240]{0,1:T(8,128)(2,1)}), bf16[8192,240]{0,1:T(8,128)(2,1)}) %all-gather.18.cloned.1.call-update) | async-done | bytes 3932176 | tf_op jit(solution)/shard_map/all_gather | solution.py:96
  276.4 4.1 convolution_convert_fusion
  280.6 29.1 %reduce-scatter.7.cloned.1.call-done = bf16[2048,120]{0,1:T(8,128)(2,1)} async-done(((bf16[8192,120]{0,1:T(8,128)(2,1)}), bf16[2048,120]{0,1:T(8,128)(2,1)}) %reduce-scatter.7.cloned.1.call-update) | async-done | bytes 491536 | tf_op jit(solution)/shard_map/reduce_scatter | solution.py:99
  310.9 30.6 %all-gather.1 = f32[16384]{0:T(1024)S(1)} all-gather(f32[2048]{0:T(1024)S(1)} %multiply_reduce_fusion), channel_id=3, replica_groups=mesh['gx'=8,'gy'=4] {'gx'}, dimensions={0}, use_global_device_ids=true | all-gather | bytes 73728 | tf_op jit(solution)/shard_map/all_gather | solution.py:18
  344.2 21.3 %all-gather.20.cloned.1.call-done = bf16[8192,120]{0,1:T(8,128)(2,1)} async-done(((bf16[2048,120]{0,1:T(8,128)(2,1)}), bf16[8192,120]{0,1:T(8,128)(2,1)}) %all-gather.20.cloned.1.call-update) | async-done | bytes 1966096 | tf_op jit(solution)/shard_map/all_gather | solution.py:89
  368.5 5.6 all-to-all-start.3
  375.0 13.8 all-gather.26.cloned.1.call-done
  388.8 3.1 copy.129
  391.9 38.2 %all-to-all-done.3 = bf16[8,1024,120]{1,2,0:T(8,128)(2,1)} async-done(((bf16[8,1024,120]{1,2,0:T(8,128)(2,1)}), bf16[8,1024,120]{1,2,0:T(8,128)(2,1)}, u32[]{:S(2)}, u32[]{:S(2)}) %all-to-all-start.3) | async-done | bytes 1966112 | tf_op jit(solution)/shard_map/all_to_all | solution.py:90
  430.0 4.3 all-to-all-start.4
  435.2 36.0 %all-gather.22.cloned.1.call-done = bf16[960,1280]{1,0:T(8,128)(2,1)} async-done(((bf16[120,1280]{1,0:T(8,128)(2,1)}), bf16[960,1280]{1,0:T(8,128)(2,1)}) %all-gather.22.cloned.1.call-update) | async-done | bytes 2457616 | tf_op jit(solution)/shard_map/all_gather | solution.py:91
  471.1 7.5 fusion.53
  478.7 45.1 %all-gather.28.cloned.1.call-done = bf16[960,640]{1,0:T(8,128)(2,1)} async-done(((bf16[120,640]{1,0:T(8,128)(2,1)}), bf16[960,640]{1,0:T(8,128)(2,1)}) %all-gather.28.cloned.1.call-update) | async-done | bytes 1228816 | tf_op jit(solution)/shard_map/all_gather | solution.py:91
  523.8 7.3 multiply_convert_fusion.1
  532.8 400.4 %all-gather.30.cloned.1.call-done = bf16[8192,1280]{1,0:T(8,128)(2,1)} async-done(((bf16[1024,1280]{1,0:T(8,128)(2,1)}), bf16[8192,1280]{1,0:T(8,128)(2,1)}) %all-gather.30.cloned.1.call-update) | async-done | bytes 20971536 | tf_op jit(solution)/shard_map/all_gather | solution.py:96
  933.3 14.8 convolution_convert_fusion.3
  948.3 30.3 %reduce-scatter.11.cloned.1.call-done = bf16[2048,120]{0,1:T(8,128)(2,1)} async-done(((bf16[8192,120]{0,1:T(8,128)(2,1)}), bf16[2048,120]{0,1:T(8,128)(2,1)}) %reduce-scatter.11.cloned.1.call-update) | async-done | bytes 491536 | tf_op jit(solution)/shard_map/reduce_scatter | solution.py:99
  980.7 32.5 %all-gather.2 = f32[16384]{0:T(1024)} all-gather(f32[2048]{0:T(1024)S(1)} %get-tuple-element.67), channel_id=4, replica_groups=mesh['gx'=8,'gy'=4] {'gx'}, dimensions={0}, use_global_device_ids=true | all-gather | bytes 73728 | tf_op jit(solution)/shard_map/all_gather | solution.py:18
  1019.1 22.0 %all-gather.32.cloned.1.call-done = bf16[8192,120]{0,1:T(8,128)(2,1)} async-done(((bf16[2048,120]{0,1:T(8,128)(2,1)}), bf16[8192,120]{0,1:T(8,128)(2,1)}) %all-gather.32.cloned.1.call-update) | async-done | bytes 1966096 | tf_op jit(solution)/shard_map/all_gather | solution.py:89
  1044.1 5.5 all-to-all-start.5
  1051.2 67.3 %all_gather.85 = bf16[960,240]{1,0:T(8,128)(2,1)} all-gather(bf16[120,240]{1,0:T(8,128)(2,1)} %bitcast.221), channel_id=1, replica_groups=mesh['gx'=8,'gy'=4] {'gx'}, dimensions={0}, use_global_device_ids=true | all-gather | bytes 518400 | tf_op jit(solution)/shard_map/all_gather | solution.py:91
  1120.9 10.9 all_to_all.138
  1131.7 8.9 fusion.13
  1140.6 7.8 fusion.54
  1148.4 25.3 %fusion.3 = bf16[5,3,256,1024]{2,3,1,0:T(8,128)(2,1)} fusion(f32[5,1024,256,3]{2,1,3,0:T(8,128)} %fusion.54, f32[5,3,256,1024]{2,3,1,0:T(8,128)} %get-tuple-element.97, f32[5,3,256]{2,1,0:T(4,128)S(1)} %log_add_fusion), kind=kOutput, calls=%fused_computation.5 | output fusion | flops 27529984 | bytes 39336960 | tf_op jit(solution)/shard_map/sub | solution.py:211
  1173.7 5.7 convolution_bitcast_fusion
  1180.6 4.7 fusion.39
  1185.5 10.9 all_to_all.139
  1196.4 5.2 reduce-scatter.13.cloned.1.call-done
  1204.2 102.1 %all-gather.34.cloned.1.call-done = bf16[8192,400]{0,1:T(8,128)(2,1)} async-done(((bf16[1024,400]{0,1:T(8,128)(2,1)}), bf16[8192,400]{0,1:T(8,128)(2,1)}) %all-gather.34.cloned.1.call-update) | async-done | bytes 6553616 | tf_op jit(solution)/shard_map/all_gather | solution.py:96
  1306.3 5.4 convolution_convert_fusion.1
  1311.8 145.3 %all-gather.24.cloned.1.call-done = bf16[8192,640]{1,0:T(8,128)(2,1)} async-done(((bf16[1024,640]{1,0:T(8,128)(2,1)}), bf16[8192,640]{1,0:T(8,128)(2,1)}) %all-gather.24.cloned.1.call-update) | async-done | bytes 10485776 | tf_op jit(solution)/shard_map/all_gather | solution.py:96
  1457.1 9.3 convolution_convert_fusion.2
  1466.4 7.2 fusion.58
  1473.6 8.9 fusion.57
  1490.1 30.5 %all-gather.3 = f32[16384]{0:T(1024)S(1)} all-gather(f32[2048]{0:T(1024)S(1)} %get-tuple-element.69), channel_id=5, replica_groups=mesh['gx'=8,'gy'=4] {'gx'}, dimensions={0}, use_global_device_ids=true | all-gather | bytes 73728 | tf_op jit(solution)/shard_map/all_gather | solution.py:18
  1520.7 6.2 all-reduce
  (169 shorter events, 55.7 us)
Async XLA Ops:
  7.2 58.5 %all-gather.16.cloned.1.call-start = ((), (), s32[]{:S(2)}) async-start(), calls=%async_computation.14 | async-start | bytes 2457600 | tf_op jit(solution)/shard_map/all_gather | solution.py:89
  68.7 5.7 copy-start.22
  68.7 6.5 copy-start.21
  68.7 6.6 copy-start.16
  68.7 6.6 copy-start.18
  68.7 76.8 %all-to-all-start = ((bf16[8,1024,120]{1,2,0:T(8,128)(2,1)}), bf16[8,1024,120]{1,2,0:T(8,128)(2,1)}, u32[]{:S(2)}, u32[]{:S(2)}) async-start(bf16[8,1024,120]{1,2,0:T(8,128)(2,1)} %bitcast.187), calls=%async_computation | async-start | bytes 3932160 | tf_op jit(solution)/shard_map/all_to_all | solution.py:90
  148.9 24.6 %all-to-all-start.1 = ((bf16[4,256,240]{1,2,0:T(8,128)(2,1)}), bf16[4,256,240]{1,2,0:T(8,128)(2,1)S(1)}, u32[]{:S(2)}, u32[]{:S(2)}) async-start(bf16[4,256,240]{1,2,0:T(8,128)(2,1)} %bitcast.189), calls=%async_computation.1 | async-start | bytes 983040 | tf_op jit(solution)/shard_map/all_to_all | solution.py:106
  152.4 124.0 %all-gather.18.cloned.1.call-start = ((), (), s32[]{:S(2)}) async-start(), calls=%async_computation.15 | async-start | bytes 4423680 | tf_op jit(solution)/shard_map/all_gather | solution.py:96
  188.2 88.2 %copy-start.12 = (bf16[240,120]{1,0:T(8,128)(2,1)S(1)}, bf16[240,120]{1,0:T(8,128)(2,1)}, u32[]{:S(2)}) copy-start(bf16[240,120]{1,0:T(8,128)(2,1)} %param.17) | copy-start | bytes 172804
  207.9 101.8 %copy-start = (bf16[120,2048]{1,0:T(8,128)(2,1)S(1)}, bf16[120,2048]{1,0:T(8,128)(2,1)}, u32[]{:S(2)}) copy-start(bf16[120,2048]{1,0:T(8,128)(2,1)} %param.12) | copy-start | bytes 1474564
  207.9 101.8 %reduce-scatter.7.cloned.1.call-start = ((), (), s32[]{:S(2)}) async-start(), calls=%async_computation.16 | async-start | bytes 2457600 | tf_op jit(solution)/shard_map/reduce_scatter | solution.py:99
  280.5 61.1 %copy-start.23 = (f32[120]{0:T(128)S(1)}, f32[120]{0:T(128)}, u32[]{:S(2)}) copy-start(f32[120]{0:T(128)} %param.18) | copy-start | bytes 1444
  280.5 85.0 %all-gather.20.cloned.1.call-start = ((), (), s32[]{:S(2)}) async-start(), calls=%async_computation.17 | async-start | bytes 2457600 | tf_op jit(solution)/shard_map/all_gather | solution.py:89
  341.5 27.0 %copy-start.20 = (f32[2048]{0:T(1024)}, f32[2048]{0:T(1024)S(1)}, u32[]{:S(2)}) copy-start(f32[2048]{0:T(1024)S(1)} %reduce_sum.112) | copy-start | bytes 24580
  343.6 45.2 %all-gather.26.cloned.1.call-start = ((), (), s32[]{:S(2)}) async-start(), calls=%async_computation.21 | async-start | bytes 2457600 | tf_op jit(solution)/shard_map/all_gather | solution.py:89
  368.5 5.7 copy-start.13
  368.5 5.7 copy-start.14
  368.5 61.5 %all-to-all-start.3 = ((bf16[8,1024,120]{1,2,0:T(8,128)(2,1)}), bf16[8,1024,120]{1,2,0:T(8,128)(2,1)}, u32[]{:S(2)}, u32[]{:S(2)}) async-start(bf16[8,1024,120]{1,2,0:T(8,128)(2,1)} %bitcast.198), calls=%async_computation.4 | async-start | bytes 3932160 | tf_op jit(solution)/shard_map/all_to_all | solution.py:90
  374.2 97.0 %all-gather.22.cloned.1.call-start = ((), (), s32[]{:S(2)}) async-start(), calls=%async_computation.18 | async-start | bytes 2764800 | tf_op jit(solution)/shard_map/all_gather | solution.py:91
  430.0 93.8 %all-to-all-start.4 = ((bf16[8,1024,120]{1,2,0:T(8,128)(2,1)}), bf16[8,1024,120]{1,2,0:T(8,128)(2,1)}, u32[]{:S(2)}, u32[]{:S(2)}) async-start(bf16[8,1024,120]{1,2,0:T(8,128)(2,1)} %bitcast.197), calls=%async_computation.6 | async-start | bytes 3932160 | tf_op jit(solution)/shard_map/all_to_all | solution.py:90
  434.4 89.4 %all-gather.28.cloned.1.call-start = ((), (), s32[]{:S(2)}) async-start(), calls=%async_computation.22 | async-start | bytes 1382400 | tf_op jit(solution)/shard_map/all_gather | solution.py:91
  435.1 498.1 %all-gather.30.cloned.1.call-start = ((), (), s32[]{:S(2)}) async-start(), calls=%async_computation.23 | async-start | bytes 23592960 | tf_op jit(solution)/shard_map/all_gather | solution.py:96
  532.8 400.5 %copy-start.9 = (bf16[120,1280]{1,0:T(8,128)(2,1)S(1)}, bf16[120,1280]{1,0:T(8,128)(2,1)}, u32[]{:S(2)}) copy-start(bf16[120,1280]{1,0:T(8,128)(2,1)} %copy-done.8) | copy-start | bytes 921604
  532.8 445.9 %copy-start.3 = (bf16[2048,120]{0,1:T(8,128)(2,1)S(1)}, bf16[2048,120]{0,1:T(8,128)(2,1)}, u32[]{:S(2)}) copy-start(bf16[2048,120]{0,1:T(8,128)(2,1)} %reduce-scatter.7.cloned.1.call-done) | copy-start | bytes 1474564
  532.8 445.8 %reduce-scatter.11.cloned.1.call-start = ((), (), s32[]{:S(2)}) async-start(), calls=%async_computation.24 | async-start | bytes 2457600 | tf_op jit(solution)/shard_map/reduce_scatter | solution.py:99
  948.1 68.8 %copy-start.6 = (bf16[120,2048]{1,0:T(8,128)(2,1)S(1)}, bf16[120,2048]{1,0:T(8,128)(2,1)}, u32[]{:S(2)}) copy-start(bf16[120,2048]{1,0:T(8,128)(2,1)} %param.23) | copy-start | bytes 1474564
  948.1 93.0 %all-gather.32.cloned.1.call-start = ((), (), s32[]{:S(2)}) async-start(), calls=%async_computation.25 | async-start | bytes 2457600 | tf_op jit(solution)/shard_map/all_gather | solution.py:89
  1044.1 74.4 %all-to-all-start.5 = ((bf16[8,1024,120]{1,2,0:T(8,128)(2,1)}), bf16[8,1024,120]{1,2,0:T(8,128)(2,1)}, u32[]{:S(2)}, u32[]{:S(2)}) async-start(bf16[8,1024,120]{1,2,0:T(8,128)(2,1)} %bitcast.199), calls=%async_computation.8 | async-start | bytes 3932160 | tf_op jit(solution)/shard_map/all_to_all | solution.py:90
  1049.6 146.8 %reduce-scatter.15.cloned.1.call-start = ((), (), s32[]{:S(2)}) async-start(), calls=%async_computation.27 | async-start | bytes 819200 | tf_op jit(solution)/shard_map/reduce_scatter | solution.py:221
  1148.3 53.3 %reduce-scatter.13.cloned.1.call-start = ((), (), s32[]{:S(2)}) async-start(), calls=%async_computation.26 | async-start | bytes 819200 | tf_op jit(solution)/shard_map/reduce_scatter | solution.py:218
  1173.7 5.7 copy-start.11
  1180.5 4.7 copy-start.15
  1180.5 125.8 %all-gather.34.cloned.1.call-start = ((), (), s32[]{:S(2)}) async-start(), calls=%async_computation.28 | async-start | bytes 7372800 | tf_op jit(solution)/shard_map/all_gather | solution.py:96
  1196.3 110.0 %copy-start.17 = (bf16[120,80]{0,1:T(8,128)(2,1)S(1)}, bf16[120,80]{0,1:T(8,128)(2,1)}, u32[]{:S(2)}) copy-start(bf16[120,80]{0,1:T(8,128)(2,1)} %param.16) | copy-start | bytes 57604
  1196.3 110.0 %copy-start.19 = (bf16[120,80]{0,1:T(8,128)(2,1)S(1)}, bf16[120,80]{0,1:T(8,128)(2,1)}, u32[]{:S(2)}) copy-start(bf16[120,80]{0,1:T(8,128)(2,1)} %param.15) | copy-start | bytes 57604
  1203.6 253.5 %all-gather.24.cloned.1.call-start = ((), (), s32[]{:S(2)}) async-start(), calls=%async_computation.19 | async-start | bytes 11796480 | tf_op jit(solution)/shard_map/all_gather | solution.py:96
  1204.2 252.9 %copy-start.10 = (bf16[640,120]{0,1:T(8,128)(2,1)S(1)}, bf16[640,120]{0,1:T(8,128)(2,1)}, u32[]{:S(2)}) copy-start(bf16[640,120]{0,1:T(8,128)(2,1)} %param.21) | copy-start | bytes 460804
  1204.2 284.4 %reduce-scatter.17.cloned.1.call-start = ((), (), s32[]{:S(2)}) async-start(), calls=%async_computation.29 | async-start | bytes 2457600 | tf_op jit(solution)/shard_map/reduce_scatter | solution.py:99
  1311.8 215.1 %reduce-scatter.9.cloned.1.call-start = ((), (), s32[]{:S(2)}) async-start(), calls=%async_computation.20 | async-start | bytes 2457600 | tf_op jit(solution)/shard_map/reduce_scatter | solution.py:99
  1466.4 7.2 copy-start.4
  1466.4 18.8 %slice-start = ((s8[6553600]{0:T(1024)(128)(4,1)}), s8[4194304]{0:T(1024)(128)(4,1)S(1)}, s32[]{:S(2)}) async-start(s8[6553600]{0:T(1024)(128)(4,1)} %bitcast.190), calls=%async_computation.30 | async-start | bytes 8388608
  1473.6 9.8 copy-start.1
  1473.6 9.8 copy-start.5
  1473.6 11.6 slice-start.1
  1485.2 3.4 copy-start.25
  1485.2 35.4 %copy-start.26 = (f32[120]{0:T(128)S(1)}, f32[120]{0:T(128)}, u32[]{:S(2)}) copy-start(f32[120]{0:T(128)} %get-tuple-element.66) | copy-start | bytes 1444
  1485.2 41.6 %copy-start.7 = (bf16[2048,120]{0,1:T(8,128)(2,1)S(1)}, bf16[2048,120]{0,1:T(8,128)(2,1)}, u32[]{:S(2)}) copy-start(bf16[2048,120]{0,1:T(8,128)(2,1)} %reduce-scatter.11.cloned.1.call-done) | copy-start | bytes 1474564
  1485.2 41.6 %copy-start.24 = (f32[120]{0:T(128)S(1)}, f32[120]{0:T(128)}, u32[]{:S(2)}) copy-start(f32[120]{0:T(128)} %param.18) | copy-start | bytes 1444
  (2 other events, 2.6 us)
Sparse Core Ops, SparseCore 0:
  42.9 22.7 all-gather.15
  208.0 68.2 all-gather.17
  280.6 28.9 reduce-scatter.6
  343.7 21.7 all-gather.19
  366.9 21.8 all-gather.25
  391.4 79.7 all-gather.21
  473.3 50.4 all-gather.27
  532.9 400.3 all-gather.29
  948.2 30.3 reduce-scatter.10
  1019.2 21.7 all-gather.31
  1148.5 20.9 reduce-scatter.14
  1180.7 20.9 reduce-scatter.12
  1204.4 101.8 all-gather.33
  1308.3 148.6 all-gather.23
  1459.5 28.5 reduce-scatter.16
  1490.5 30.3 reduce-scatter.8
